TPU v7x, 32 devices: a whole 2x2x4 slice. The times are simulated.
32 devices in a mesh: expert: 4 (over z), shard: 8 (over y, x, core).
Axes of the slice: x: 2, y: 2, z: 4, core: 2. Of those that a mesh axis runs over, the one named last changes fastest.
Arguments:
- master_gate: float32 [64, 2048, 1024], P('expert', 'shard'), may hold values from -0.1875 to 0.1875
- second_gate: float32 [64, 2048, 1024], P('expert', 'shard'), may hold values from -0.125 to 0.125
- master_up: float32 [64, 2048, 1024], P('expert', 'shard'), may hold values from -0.1875 to 0.1875
- second_up: float32 [64, 2048, 1024], P('expert', 'shard'), may hold values from -0.125 to 0.125
- mix_share: float32 [64], P('expert'), may hold values from 0.2 to 0.8
- router_weight: float32 [2048, 64], P('shard', 'expert'), may hold values from -0.125 to 0.125
- router_gain: float32 [2048], P('shard'), may hold values from 0.25 to 1.75
Outputs:
- final_gate: bfloat16 [64, 2048, 1024], P('expert', None, 'shard')
- final_up: bfloat16 [64, 2048, 1024], P('expert', None, 'shard')
- scale_gate: float32 [64, 1024], P('expert', 'shard')
- scale_up: float32 [64, 1024], P('expert', 'shard')
- serve_router: bfloat16 [2048, 64], replicated
All inputs are finite; a program needn't handle non-finite values.
Results may differ from a plain program's by a relative error of at most 0.001.
Values may be sent and summed in bfloat16 or wider, within the bound.
A program may use at most 256 MiB of HBM per device.

v0:
```python
import jax
import jax.numpy as jnp
from jax import lax
from jax.sharding import PartitionSpec as P

D_MODEL = 2048


def local(master_gate, second_gate, master_up, second_up, mix_share, router_weight, router_gain):
    merged_gate = (
        mix_share[:, None, None] * master_gate + (1.0 - mix_share[:, None, None]) * second_gate
    )
    merged_up = mix_share[:, None, None] * master_up + (1.0 - mix_share[:, None, None]) * second_up
    total_gate, total_up = lax.psum(
        (jnp.sum(jnp.abs(merged_gate), axis=1), jnp.sum(jnp.abs(merged_up), axis=1)), "shard"
    )
    scale_gate = total_gate / D_MODEL
    scale_up = total_up / D_MODEL
    narrow_gate, narrow_up = (
        (merged_gate / jnp.expand_dims(scale_gate, 1)).astype(jnp.bfloat16),
        (merged_up / jnp.expand_dims(scale_up, 1)).astype(jnp.bfloat16),
    )
    final_gate, final_up = (
        lax.all_to_all(narrow_gate, "shard", split_axis=2, concat_axis=1, tiled=True),
        lax.all_to_all(narrow_up, "shard", split_axis=2, concat_axis=1, tiled=True),
    )
    scale_gate = lax.dynamic_slice_in_dim(
        scale_gate, lax.axis_index("shard") * final_gate.shape[2], final_gate.shape[2], axis=1
    )
    scale_up = lax.dynamic_slice_in_dim(
        scale_up, lax.axis_index("shard") * final_up.shape[2], final_up.shape[2], axis=1
    )
    part_router = (router_weight * router_gain[:, None]).astype(jnp.bfloat16)
    row_router = lax.all_gather(part_router, "shard", axis=0, tiled=True)
    serve_router = lax.all_gather(row_router, "expert", axis=1, tiled=True)
    return (final_gate, final_up, scale_gate, scale_up, serve_router)


def solution(mesh):
    placed = (
        P("expert", "shard", None),
        P("expert", "shard", None),
        P("expert", "shard", None),
        P("expert", "shard", None),
        P("expert"),
        P("shard", "expert"),
        P("shard"),
    )
    return jax.shard_map(
        local,
        mesh=mesh,
        in_specs=placed,
        out_specs=(
            P("expert", None, "shard"),
            P("expert", None, "shard"),
            P("expert", "shard"),
            P("expert", "shard"),
            P(),
        ),
        check_vma=False,
    )
```

profile of v0, /device:TPU:0, one launch (start us, length us, event | category | flops | bytes accessed | tf_op | source)
XLA Modules:
  0.0 434.9 jit_solution(18230987575285412976)
XLA Ops:
  7.2 0.0 all-reduce.3.cloned.1.call-start
  7.2 17.6 %copy.22 = f32[16,256,1024]{1,0,2:T(8,128)} copy(f32[16,256,1024]{2,1,0:T(8,128)} %param.7) | data formatting | bytes 33554432 | tf_op args[0]
  24.8 17.6 %copy.23 = f32[16,256,1024]{1,0,2:T(8,128)} copy(f32[16,256,1024]{2,1,0:T(8,128)} %param.8) | data formatting | bytes 33554432 | tf_op args[1]
  42.4 17.6 %copy.25 = f32[16,256,1024]{1,0,2:T(8,128)} copy(f32[16,256,1024]{2,1,0:T(8,128)} %param.9) | data formatting | bytes 33554432 | tf_op args[2]
  60.0 0.0 copy-start.1
  60.0 17.6 %copy.26 = f32[16,256,1024]{1,0,2:T(8,128)} copy(f32[16,256,1024]{2,1,0:T(8,128)} %param.10) | data formatting | bytes 33554432 | tf_op args[3]
  77.6 0.0 copy-done.1
  77.6 23.7 %abs_reduce_fusion = (f32[16,1024]{0,1:T(8,128)}, f32[16,1024]{0,1:T(8,128)}) fusion(f32[16,256,1024]{1,0,2:T(8,128)} %copy.26, f32[16]{0:T(128)S(1)} %broadcast_subtract_fusion, f32[16,256,1024]{1,0,2:T(8,128)} %copy.25, f32[16]{0:T(128)S(1)} %copy-done.1, f32[16,256,1024]{1,0,2:T(8,128)} %copy.23, f32[16,256,1024]{1,0,2:T(8,128)} %copy.22), kind=kLoop, calls=%fused_computation.1 | loop fusion | flops 41910272 | bytes 67240064 | tf_op jit(solution)/shard_map/reduce_sum | solution.py:15
  101.3 0.0 all-reduce.3.cloned.1.call-update
  101.4 59.7 %all-reduce.3.cloned.1.call-done = (f32[16,1024]{0,1:T(8,128)}, f32[16,1024]{0,1:T(8,128)}) async-done(((f32[16,1024]{0,1:T(8,128)}, f32[16,1024]{0,1:T(8,128)}), (f32[16,1024]{0,1:T(8,128)}, f32[16,1024]{0,1:T(8,128)})) %all-reduce.3.cloned.1.call-update) | async-done | bytes 131088 | tf_op jit(solution)/shard_map/psum | solution.py:14
  161.0 1.3 broadcast_multiply_fusion
  162.3 25.3 %divide_convert_fusion = (bf16[16,256,1024]{1,0,2:T(8,128)(2,1)}, bf16[16,256,1024]{1,0,2:T(8,128)(2,1)S(1)}) fusion(f32[16,1024]{0,1:T(8,128)S(1)} %get-tuple-element.16, f32[16,256,1024]{1,0,2:T(8,128)} %copy.26, f32[16]{0:T(128)S(1)} %broadcast_subtract_fusion, f32[16,256,1024]{1,0,2:T(8,128)} %copy.25, f32[16]{0:T(128)S(1)} %copy-done.1, ...), kind=kLoop, calls=%fused_computation | loop fusion | flops 41943040 | bytes 84017280 | tf_op jit(solution)/shard_map/convert_element_type | solution.py:21
  187.6 0.0 copy-start
  187.6 0.0 copy-start.2
  187.6 97.6 %all_to_all.36 = bf16[16,256,1024]{1,0,2:T(8,128)(2,1)} all-to-all(bf16[16,256,1024]{1,0,2:T(8,128)(2,1)S(1)} %get-tuple-element.15), channel_id=1, replica_groups=mesh['expert'=4,'shard'=8] {'shard'}, dimensions={2} | all-to-all | bytes 16777216 | tf_op jit(solution)/shard_map/all_to_all | solution.py:24
  285.2 4.9 %all-to-all-start.1 = ((bf16[16,256,1024]{1,0,2:T(8,128)(2,1)}), bf16[16,256,1024]{1,0,2:T(8,128)(2,1)}, u32[]{:S(2)}, u32[]{:S(2)}) async-start(bf16[16,256,1024]{1,0,2:T(8,128)(2,1)} %get-tuple-element.14), calls=%async_computation.1 | async-start | bytes 16777216 | tf_op jit(solution)/shard_map/all_to_all | solution.py:25
  290.2 0.0 copy-done
  290.2 0.0 copy-done.2
  290.2 97.3 %all_gather.6 = bf16[2048,16]{0,1:T(8,128)(2,1)S(1)} all-gather(bf16[256,16]{0,1:T(8,128)(2,1)S(1)} %multiply_convert_fusion), channel_id=1, replica_groups=mesh['expert'=4,'shard'=8] {'shard'}, dimensions={0}, use_global_device_ids=true | all-gather | bytes 73728 | tf_op jit(solution)/shard_map/all_gather | solution.py:34
  387.6 13.9 %all_gather.7 = bf16[2048,64]{0,1:T(8,128)(2,1)S(1)} all-gather(bf16[2048,16]{0,1:T(8,128)(2,1)S(1)} %all_gather.6), channel_id=1, replica_groups=mesh['expert'=4,'shard'=8] {'expert'}, dimensions={1}, use_global_device_ids=true | all-gather | bytes 327680 | tf_op jit(solution)/shard_map/all_gather | solution.py:35
  401.4 0.7 copy.28
  402.1 0.7 copy.29
  402.8 12.3 %copy.24 = bf16[16,8,256,128]{3,2,1,0:T(8,128)(2,1)} copy(bf16[16,8,256,128]{2,0,3,1:T(8,128)(2,1)} %bitcast.8) | data formatting | bytes 16777216 | tf_op jit(solution)/shard_map/all_to_all | solution.py:24
  415.0 0.0 all-to-all-done.1
  415.0 12.3 %copy.27 = bf16[16,8,256,128]{3,2,1,0:T(8,128)(2,1)} copy(bf16[16,8,256,128]{2,0,3,1:T(8,128)(2,1)} %bitcast.4) | data formatting | bytes 16777216 | tf_op jit(solution)/shard_map/all_to_all | solution.py:25
  427.3 0.7 copy.33
  (4 shorter events, 0.0 us)
Async XLA Ops:
  7.2 153.9 %all-reduce.3.cloned.1.call-start = ((), (), s32[]{:S(2)}) async-start(), calls=%async_computation.2 | async-start | bytes 2097152 | tf_op jit(solution)/shard_map/psum | solution.py:14
  60.0 17.6 %copy-start.1 = (f32[16]{0:T(128)S(1)}, f32[16]{0:T(128)}, u32[]{:S(2)}) copy-start(f32[16]{0:T(128)} %param.11) | copy-start | bytes 196
  187.6 102.6 %copy-start = (f32[256,16]{0,1:T(8,128)S(1)}, f32[256,16]{0,1:T(8,128)}, u32[]{:S(2)}) copy-start(f32[256,16]{0,1:T(8,128)} %param.12) | copy-start | bytes 49156
  187.6 102.6 %copy-start.2 = (f32[256]{0:T(256)S(1)}, f32[256]{0:T(256)}, u32[]{:S(2)}) copy-start(f32[256]{0:T(256)} %param.13) | copy-start | bytes 3076
  285.2 129.8 %all-to-all-start.1 = ((bf16[16,256,1024]{1,0,2:T(8,128)(2,1)}), bf16[16,256,1024]{1,0,2:T(8,128)(2,1)}, u32[]{:S(2)}, u32[]{:S(2)}) async-start(bf16[16,256,1024]{1,0,2:T(8,128)(2,1)} %get-tuple-element.14), calls=%async_computation.1 | async-start | bytes 16777216 | tf_op jit(solution)/shard_map/all_to_all | solution.py:25
Sparse Core Ops, SparseCore 0:
  101.5 59.4 all-reduce.2
where the time goes:
time: 437 us; the launch traced here: 435 us
  blocking collectives  209 us (48%)
  local copies, waits for them, and re-layouts  97 us (22%)
  waiting for transfers between devices  59.7 us (14%)
  other arithmetic  50.3 us (12%)
  between operations  14.1 us (3%)
  starting transfers between devices  4.98 us (1%)
    all_to_all x1, blocking collectives, local(): lax.all_to_all(narrow_gate, 'shard', split_axis=2, concat_axis=1, tiled=T...  97.6 us
    all_gather x1, blocking collectives, local(): row_router = lax.all_gather(part_router, 'shard', axis=0, tiled=True)  97.3 us
    unnamed x13, local copies, waits for them, and re-layouts  72.5 us
    psum x1, waiting for transfers between devices, local(): lax.psum((jnp.sum(jnp.abs(merged_gate), axis=1), jnp.sum(jnp.abs(merged_u...  59.7 us
    convert_element_type x1, other arithmetic, local(): (merged_up / jnp.expand_dims(scale_up, 1)).astype(jnp.bfloat16)  25.3 us
    reduce_sum x1, other arithmetic, local(): jnp.sum(jnp.abs(merged_up), axis=1)  23.7 us
    all_gather x1, blocking collectives, local(): serve_router = lax.all_gather(row_router, 'expert', axis=1, tiled=True)  13.9 us
    all_to_all x1, local copies, waits for them, and re-layouts, local(): lax.all_to_all(narrow_up, 'shard', split_axis=2, concat_axis=1, tiled=True)  12.3 us
  transfers between devices with their start and end apart: 2, of which 1 were waited for; matrix products, arithmetic and copies ran while one was open for 3% of the time, Pallas kernels for 0%

commit v1 on v0

v1 whole, which is shorter than its diff:
```python
import functools

import jax
import jax.numpy as jnp
from jax import lax
from jax.experimental import pallas as pl
from jax.experimental.pallas import tpu as pltpu
from jax.sharding import PartitionSpec as P

LANES = 128
LOAD_SLOTS = 3
SUM_LAG = 1
SCALE_LAG = 1
KEPT = SUM_LAG + SCALE_LAG + 1


def plain(width, master_gate, second_gate, master_up, second_up, mix_share, router_weight, router_gain):
    share = mix_share[:, None, None]
    merged_gate = share * master_gate + (1.0 - share) * second_gate
    merged_up = share * master_up + (1.0 - share) * second_up
    total_gate, total_up = lax.psum(
        (jnp.sum(jnp.abs(merged_gate), axis=1), jnp.sum(jnp.abs(merged_up), axis=1)), "shard"
    )
    rows = master_gate.shape[1] * lax.axis_size("shard")
    finals, scales = [], []
    for merged, total in ((merged_gate, total_gate), (merged_up, total_up)):
        scale = total / rows
        narrow = (merged / jnp.expand_dims(scale, 1)).astype(jnp.bfloat16)
        finals.append(lax.all_to_all(narrow, "shard", split_axis=2, concat_axis=1, tiled=True))
        scales.append(
            lax.dynamic_slice_in_dim(scale, lax.axis_index("shard") * width, width, axis=1)
        )
    part_router = (router_weight * router_gain[:, None]).astype(jnp.bfloat16)
    row_router = lax.all_gather(part_router, "shard", axis=0, tiled=True)
    serve_router = lax.all_gather(row_router, "expert", axis=1, tiled=True)
    return (*finals, *scales, serve_router)


def partner(me, k):
    other, bit = me, 1
    while bit <= k:
        if k & bit:
            other = other + bit * (1 - 2 * ((me // bit) % 2))
        bit *= 2
    return other


def kernel(
    n, groups, order,
    mix, mg, sg, mu, su, rw, rg,
    out_g, out_u, sc_g, sc_u, out_r,
    loaded, merged, stage, sums, sums_in, scale_out, scales_in,
    load_sem, small_send, sum_sem, scale_sem, bulk_send, bulk_g, bulk_u, own_sem,
    r_send, r_plane, r_group,
):
    experts, rows, cols = mg.shape
    width = cols // n
    total_rows = rows * n
    me = lax.axis_index("shard")
    group = lax.axis_index("expert")
    sources = (mg, sg, mu, su)

    barrier = pltpu.get_barrier_semaphore()
    for k in range(1, n):
        pl.semaphore_signal(barrier, inc=1, device_id={"shard": partner(me, k)})
    for k in range(1, groups):
        pl.semaphore_signal(barrier, inc=1, device_id={"expert": lax.rem(group + k, groups)})

    def load(e, which=(0, 1, 2, 3)):
        slot = lax.rem(e, LOAD_SLOTS)
        return [
            pltpu.make_async_copy(sources[j].at[e], loaded.at[slot, j], load_sem.at[slot, j])
            for j in which
        ]

    for e in range(min(LOAD_SLOTS, experts)):
        for copy in load(e):
            copy.start()
    pl.semaphore_wait(barrier, n - 1 + groups - 1)

    def remote(src, dst, send, recv, k):
        return pltpu.make_async_remote_copy(
            src_ref=src, dst_ref=dst, send_sem=send, recv_sem=recv,
            device_id={"shard": partner(me, k)},
        )

    def mix_and_sum(e):
        slot, keep = lax.rem(e, LOAD_SLOTS), lax.rem(e, KEPT)
        m = mix[e]
        rest = 1.0 - m
        step = 16
        for t in range(2):
            for copy in load(e, (2 * t, 2 * t + 1)):
                copy.wait()

            def tile(r, acc):
                at = pl.ds(pl.multiple_of(r * step, step), step)
                value = m * loaded[slot, 2 * t, at, :] + rest * loaded[slot, 2 * t + 1, at, :]
                merged[keep, t, at, :] = value
                size = jnp.abs(value)
                return acc + size[:8] + size[8:]

            acc = lax.fori_loop(0, rows // step, tile, jnp.zeros((8, cols), jnp.float32))
            total = jnp.sum(acc, axis=0, keepdims=True)
            for d in range(n):
                sums[e, d, t : t + 1, :] = total[:, d * width : (d + 1) * width]
        sums_in[e, 0] = sums[e, me]
        for k in order:
            remote(sums.at[e, partner(me, k)], sums_in.at[e, k], small_send.at[0], sum_sem.at[e], k).start()

        @pl.when(e + LOAD_SLOTS < experts)
        def _():
            for copy in load(e + LOAD_SLOTS):
                copy.start()

    def settle(e):
        arrived = sums_in.at[e, pl.ds(1, n - 1)]
        pltpu.make_async_copy(arrived, arrived, sum_sem.at[e]).wait()
        scale = jnp.sum(sums_in[e], axis=0) / total_rows
        scale_out[e] = scale
        scales_in[e, 0] = scale
        sc_g[pl.ds(e, 1), :] = scale[0:1]
        sc_u[pl.ds(e, 1), :] = scale[1:2]
        for k in order:
            remote(scale_out.at[e], scales_in.at[e, k], small_send.at[1], scale_sem.at[e], k).start()

    def narrow_and_send(e):
        keep = lax.rem(e, KEPT)
        arrived = scales_in.at[e, pl.ds(1, n - 1)]
        pltpu.make_async_copy(arrived, arrived, scale_sem.at[e]).wait()
        place = pl.ds(pl.multiple_of(me * rows, rows), rows)
        for t, out, sem in ((0, out_g, bulk_g), (1, out_u, bulk_u)):
            for k in (*order, 0):
                at = pl.ds(pl.multiple_of(partner(me, k) * width, width), width)
                scale = scales_in[e, k, t : t + 1, :]
                stage[e, t, k] = (merged[keep, t, :, at] / scale).astype(jnp.bfloat16)
            for k in order:
                remote(stage.at[e, t, k], out.at[e, place], bulk_send.at[t], sem, k).start()
            pltpu.make_async_copy(stage.at[e, t, 0], out.at[e, place], own_sem.at[t]).start()

    height = rw.shape[0]
    high = pl.ds(pl.multiple_of(group * height, height), height)

    def router_plane():
        mine = out_r.at[high, pl.ds(pl.multiple_of(me * rows, rows), rows)]
        mine[...] = (rw[...] * rg[...]).astype(jnp.bfloat16)
        for k in order:
            remote(mine, mine, r_send.at[0], r_plane, k).start()

    def router_groups():
        arrived = out_r.at[high, pl.ds(0, (n - 1) * rows)]
        pltpu.make_async_copy(arrived, arrived, r_plane).wait()
        for k in range(1, groups):
            pltpu.make_async_remote_copy(
                src_ref=out_r.at[high], dst_ref=out_r.at[high],
                send_sem=r_send.at[1], recv_sem=r_group,
                device_id={"expert": lax.rem(group + k, groups)},
            ).start()

    last = experts + SUM_LAG + SCALE_LAG - 1

    @pl.loop(0, last + 1)
    def _(i):
        @pl.when(i < experts)
        def _():
            mix_and_sum(i)

        @pl.when((i >= SUM_LAG) & (i < experts + SUM_LAG))
        def _():
            settle(i - SUM_LAG)

        @pl.when(i >= SUM_LAG + SCALE_LAG)
        def _():
            narrow_and_send(i - SUM_LAG - SCALE_LAG)

        @pl.when(i == SUM_LAG + SCALE_LAG)
        def _():
            router_plane()

        @pl.when(i == last)
        def _():
            router_groups()

    def finish(ref, sem):
        pltpu.make_async_copy(ref, ref, sem).wait()

    others = pl.ds(0, (n - 1) * rows)
    for t, half in enumerate((sums_in, scales_in)):
        finish(half.at[:, pl.ds(1, n - 1)], small_send.at[t])
    finish(out_r.at[pl.ds(0, height), others], r_send.at[0])
    if groups > 1:
        for sem in (r_send.at[1], r_group):
            finish(out_r.at[pl.ds(0, (groups - 1) * height)], sem)
    for t, (out, sem) in enumerate(((out_g, bulk_g), (out_u, bulk_u))):
        finish(out.at[:, others], bulk_send.at[t])
        finish(out.at[:, pl.ds(0, rows)], own_sem.at[t])
        finish(out.at[:, others], sem)


def fused(n, groups, master_gate, second_gate, master_up, second_up, mix_share, router_weight, router_gain):
    experts, rows, cols = master_gate.shape
    width = cols // n
    per_group = router_weight.shape[1]
    order = sorted(range(1, n), key=lambda k: (k // 2 == 0, -bin(k // 2).count("1"), k % 2, k))
    f32, bf16 = jnp.float32, jnp.bfloat16
    final = jax.ShapeDtypeStruct((experts, rows * n, width), bf16)
    scale = jax.ShapeDtypeStruct((experts, width), f32)
    anywhere = pl.BlockSpec(memory_space=pl.ANY)
    vmem = pl.BlockSpec(memory_space=pltpu.VMEM)
    final_gate, final_up, scale_gate, scale_up, router = pl.pallas_call(
        functools.partial(kernel, n, groups, order),
        out_shape=(
            final, final, scale, scale,
            jax.ShapeDtypeStruct((groups * per_group, n * rows), bf16),
        ),
        in_specs=[pl.BlockSpec(memory_space=pltpu.SMEM)] + [anywhere] * 4 + [vmem] * 2,
        out_specs=(anywhere, anywhere, vmem, vmem, vmem),
        scratch_shapes=[
            pltpu.VMEM((LOAD_SLOTS, 4, rows, cols), f32),
            pltpu.VMEM((KEPT, 2, rows, cols), f32),
            pltpu.VMEM((experts, 2, n, rows, width), bf16),
            pltpu.VMEM((experts, n, 2, width), f32),
            pltpu.VMEM((experts, n, 2, width), f32),
            pltpu.VMEM((experts, 2, width), f32),
            pltpu.VMEM((experts, n, 2, width), f32),
            pltpu.SemaphoreType.DMA((LOAD_SLOTS, 4)),
            pltpu.SemaphoreType.DMA((2,)),
            pltpu.SemaphoreType.DMA((experts,)),
            pltpu.SemaphoreType.DMA((experts,)),
            pltpu.SemaphoreType.DMA((2,)),
            pltpu.SemaphoreType.DMA,
            pltpu.SemaphoreType.DMA,
            pltpu.SemaphoreType.DMA((2,)),
            pltpu.SemaphoreType.DMA((2,)),
            pltpu.SemaphoreType.DMA,
            pltpu.SemaphoreType.DMA,
        ],
        compiler_params=pltpu.CompilerParams(
            collective_id=0, has_side_effects=True, vmem_limit_bytes=60 * 1024 * 1024
        ),
    )(
        mix_share, master_gate, second_gate, master_up, second_up,
        router_weight.T, router_gain[None, :],
    )
    return final_gate, final_up, scale_gate, scale_up, router.T


def solution(mesh):
    n, groups = mesh.shape["shard"], mesh.shape["expert"]

    def local(master_gate, *rest):
        width = master_gate.shape[2] // n
        whole_lanes = width % LANES == 0 and n & (n - 1) == 0 and n > 1 and master_gate.shape[1] % 16 == 0
        if whole_lanes:
            return fused(n, groups, master_gate, *rest)
        return plain(width, master_gate, *rest)

    return jax.shard_map(
        local,
        mesh=mesh,
        in_specs=(
            P("expert", "shard", None),
            P("expert", "shard", None),
            P("expert", "shard", None),
            P("expert", "shard", None),
            P("expert"),
            P("shard", "expert"),
            P("shard"),
        ),
        out_specs=(
            P("expert", None, "shard"),
            P("expert", None, "shard"),
            P("expert", "shard"),
            P("expert", "shard"),
            P(),
        ),
        check_vma=False,
    )
```

time: 437 us -> 218 us (0.50)
  blocking collectives: 209 us -> 0 us
  Pallas kernels: 0 us -> 200 us
  local copies, waits for them, and re-layouts: 97 us -> 17.1 us
  waiting for transfers between devices: 59.7 us -> 0 us
  other arithmetic: 50.3 us -> 0 us
  between operations: 14.1 us -> 0.67 us
  starting transfers between devices: 4.98 us -> 0 us
    pallas_call x0 -> x1, Pallas kernels: none -> 200 us  [fused(): pl.pallas_call(functools.partial(kernel, n, groups, order), out_shape=(fi...]
    all_gather x2 -> x0, blocking collectives: 111 us -> none  [the longest x1 97.3 us: local(): row_router = lax.all_gather(part_router, 'shard', axis=0, tiled=True)]
    all_to_all x1 -> x0, blocking collectives: 97.6 us -> none  [local(): lax.all_to_all(narrow_gate, 'shard', split_axis=2, concat_axis=1, tiled=T...]
    psum x1 -> x0, waiting for transfers between devices: 59.7 us -> none  [local(): lax.psum((jnp.sum(jnp.abs(merged_gate), axis=1), jnp.sum(jnp.abs(merged_u...]
    unnamed x13 -> x11, local copies, waits for them, and re-layouts: 72.5 us -> 17.1 us
    convert_element_type x2 -> x0, other arithmetic: 25.3 us -> none  [the longest x1 25.3 us: local(): (merged_up / jnp.expand_dims(scale_up, 1)).astype(jnp.bfloat16)]
    all_to_all x2 -> x0, local copies, waits for them, and re-layouts: 24.6 us -> none  [the longest x1 12.3 us: local(): lax.all_to_all(narrow_up, 'shard', split_axis=2, concat_axis=1, tiled=True)]
    reduce_sum x1 -> x0, other arithmetic: 23.7 us -> none  [local(): jnp.sum(jnp.abs(merged_up), axis=1)]
  transfers between devices with their start and end apart: 2 -> 0, of which waited for: 1 -> 0; matrix products, arithmetic and copies ran while one was open for 3% -> 0% of each run, Pallas kernels for 0% -> 0%
where the time goes in v1:
time: 218 us; the launch traced here: 217 us
  Pallas kernels  200 us (92%)
  local copies, waits for them, and re-layouts  17.1 us (8%)
    pallas_call x1, Pallas kernels, fused(): pl.pallas_call(functools.partial(kernel, n, groups, order), out_shape=(fi...  200 us
    unnamed x11, local copies, waits for them, and re-layouts  17.1 us

profile of v1, /device:TPU:0, one launch (start us, length us, event | category | flops | bytes accessed | tf_op | source)
XLA Modules:
  0.0 217.4 jit_solution(1873357173163646821)
XLA Ops:
  0.6 199.6 %shard_map.110 = (bf16[16,2048,128]{2,1,0:T(8,128)(2,1)}, bf16[16,2048,128]{2,1,0:T(8,128)(2,1)}, f32[16,128]{1,0:T(8,128)}, f32[16,128]{1,0:T(8,128)}, bf16[64,2048]{1,0:T(8,128)(2,1)}) custom-call(f32[16]{0:T(128)} %mix.1, f32[16,256,1024]{2,1,0:T(8,128)} %mg.1, f32[16,256,1024]{2,1,0:T(8,128)} %sg.1, f32[16,256,1024]{2,1,0:T(8,128)} %mu.1, ...), custom_call_target="tpu_custom_call" | custom-call | tf_op jit(solution)/shard_map/pallas_call | solution.py:210
  200.2 0.0 copy-start.2
  200.2 0.0 copy-start.1
  200.2 0.0 copy-start
  200.2 7.6 %copy.17 = bf16[16,2048,128]{2,1,0:T(8,128)(2,1)} copy(bf16[16,2048,128]{2,1,0:T(8,128)(2,1)} %get-tuple-element.20) | data formatting | bytes 16777216
  207.9 7.6 %copy.18 = bf16[16,2048,128]{2,1,0:T(8,128)(2,1)} copy(bf16[16,2048,128]{2,1,0:T(8,128)(2,1)} %get-tuple-element.21) | data formatting | bytes 16777216
  215.5 0.0 copy-done.2
  215.5 0.6 copy.19
  216.1 0.0 copy-done.1
  216.1 0.6 copy.20
  216.7 0.0 copy-done
  216.7 0.7 copy.21
Async XLA Ops:
  200.2 15.2 %copy-start.2 = (f32[16,128]{1,0:T(8,128)S(1)}, f32[16,128]{1,0:T(8,128)}, u32[]{:S(2)}) copy-start(f32[16,128]{1,0:T(8,128)} %get-tuple-element.22) | copy-start | bytes 24580
  200.2 15.8 %copy-start.1 = (f32[16,128]{1,0:T(8,128)S(1)}, f32[16,128]{1,0:T(8,128)}, u32[]{:S(2)}) copy-start(f32[16,128]{1,0:T(8,128)} %get-tuple-element.23) | copy-start | bytes 24580
  200.2 16.4 %copy-start = (bf16[64,2048]{1,0:T(8,128)(2,1)S(1)}, bf16[64,2048]{1,0:T(8,128)(2,1)}, u32[]{:S(2)}) copy-start(bf16[64,2048]{1,0:T(8,128)(2,1)} %get-tuple-element.14) | copy-start | bytes 786436

commit v2 on v1

--- a/solution.py
+++ b/solution.py
@@ -50,7 +50,7 @@
     mix, mg, sg, mu, su, rw, rg,
     out_g, out_u, sc_g, sc_u, out_r,
     loaded, merged, stage, sums, sums_in, scale_out, scales_in,
-    load_sem, small_send, sum_sem, scale_sem, bulk_send, bulk_g, bulk_u, own_sem,
+    load_sem, small_send, sum_sem, scale_sem, bulk_send, bulk_g, bulk_u,
     r_send, r_plane, r_group,
 ):
     experts, rows, cols = mg.shape
@@ -133,10 +133,13 @@
             for k in (*order, 0):
                 at = pl.ds(pl.multiple_of(partner(me, k) * width, width), width)
                 scale = scales_in[e, k, t : t + 1, :]
-                stage[e, t, k] = (merged[keep, t, :, at] / scale).astype(jnp.bfloat16)
+                narrow = (merged[keep, t, :, at] / scale).astype(jnp.bfloat16)
+                if k:
+                    stage[e, t, k - 1] = narrow
+                else:
+                    out[e, place, :] = narrow
             for k in order:
-                remote(stage.at[e, t, k], out.at[e, place], bulk_send.at[t], sem, k).start()
-            pltpu.make_async_copy(stage.at[e, t, 0], out.at[e, place], own_sem.at[t]).start()
+                remote(stage.at[e, t, k - 1], out.at[e, place], bulk_send.at[t], sem, k).start()
 
     height = rw.shape[0]
     high = pl.ds(pl.multiple_of(group * height, height), height)
@@ -193,7 +196,6 @@
             finish(out_r.at[pl.ds(0, (groups - 1) * height)], sem)
     for t, (out, sem) in enumerate(((out_g, bulk_g), (out_u, bulk_u))):
         finish(out.at[:, others], bulk_send.at[t])
-        finish(out.at[:, pl.ds(0, rows)], own_sem.at[t])
         finish(out.at[:, others], sem)
 
 
@@ -203,7 +205,7 @@
     per_group = router_weight.shape[1]
     order = sorted(range(1, n), key=lambda k: (k // 2 == 0, -bin(k // 2).count("1"), k % 2, k))
     f32, bf16 = jnp.float32, jnp.bfloat16
-    final = jax.ShapeDtypeStruct((experts, rows * n, width), bf16)
+    final = pltpu.VMEM((experts, rows * n, width), bf16)
     scale = jax.ShapeDtypeStruct((experts, width), f32)
     anywhere = pl.BlockSpec(memory_space=pl.ANY)
     vmem = pl.BlockSpec(memory_space=pltpu.VMEM)
@@ -214,11 +216,11 @@
             jax.ShapeDtypeStruct((groups * per_group, n * rows), bf16),
         ),
         in_specs=[pl.BlockSpec(memory_space=pltpu.SMEM)] + [anywhere] * 4 + [vmem] * 2,
-        out_specs=(anywhere, anywhere, vmem, vmem, vmem),
+        out_specs=(vmem,) * 5,
         scratch_shapes=[
             pltpu.VMEM((LOAD_SLOTS, 4, rows, cols), f32),
             pltpu.VMEM((KEPT, 2, rows, cols), f32),
-            pltpu.VMEM((experts, 2, n, rows, width), bf16),
+            pltpu.VMEM((experts, 2, n - 1, rows, width), bf16),
             pltpu.VMEM((experts, n, 2, width), f32),
             pltpu.VMEM((experts, n, 2, width), f32),
             pltpu.VMEM((experts, 2, width), f32),
@@ -231,12 +233,11 @@
             pltpu.SemaphoreType.DMA,
             pltpu.SemaphoreType.DMA,
             pltpu.SemaphoreType.DMA((2,)),
-            pltpu.SemaphoreType.DMA((2,)),
             pltpu.SemaphoreType.DMA,
             pltpu.SemaphoreType.DMA,
         ],
         compiler_params=pltpu.CompilerParams(
-            collective_id=0, has_side_effects=True, vmem_limit_bytes=60 * 1024 * 1024
+            collective_id=0, has_side_effects=True, vmem_limit_bytes=36 * 2**20
         ),
     )(
         mix_share, master_gate, second_gate, master_up, second_up,

time: 218 us -> 210 us (0.963)
  local copies, waits for them, and re-layouts: 17.1 us -> 10.7 us
    unnamed x11, local copies, waits for them, and re-layouts: 17.1 us -> 10.7 us
where the time goes in v2:
time: 210 us
  Pallas kernels  199 us (95%)
  local copies, waits for them, and re-layouts  10.7 us (5%)
    pallas_call x1, Pallas kernels, fused(): pl.pallas_call(functools.partial(kernel, n, groups, order), out_shape=(fi...  199 us
    unnamed x11, local copies, waits for them, and re-layouts  10.7 us

profile of v2, /device:TPU:0, one launch (start us, length us, event | category | flops | bytes accessed | tf_op | source)
XLA Modules:
  0.0 210.0 jit_solution(3139226837844866888)
XLA Ops:
  0.6 0.0 copy-start
  0.6 0.7 copy-done
  1.4 0.0 copy-start.1
  1.4 0.7 copy-done.1
  2.0 0.0 copy-start.2
  2.0 0.7 copy-done.2
  2.7 198.6 %shard_map.110 = (bf16[16,2048,128]{2,1,0:T(8,128)(2,1)S(1)}, bf16[16,2048,128]{2,1,0:T(8,128)(2,1)S(1)}, f32[16,128]{1,0:T(8,128)S(1)}, f32[16,128]{1,0:T(8,128)S(1)}, bf16[64,2048]{1,0:T(8,128)(2,1)S(1)}) custom-call(f32[16]{0:T(128)S(1)} %copy-done.2, f32[16,256,1024]{2,1,0:T(8,128)} %mg.1, f32[16,256,1024]{2,1,0:T(8,128)} %sg.1, f32[16,256,1024]{2,1,0:T(8,128)} %mu.1, ...), custom_call_target="tpu_custom_call" | custom-call | tf_op jit(solution)/shard_map/pallas_call | solution.py:212
  201.3 3.4 %copy.17 = bf16[16,2048,128]{2,1,0:T(8,128)(2,1)} copy(bf16[16,2048,128]{2,1,0:T(8,128)(2,1)S(1)} %get-tuple-element.15) | data formatting | bytes 16777216
  204.7 3.4 %copy.18 = bf16[16,2048,128]{2,1,0:T(8,128)(2,1)} copy(bf16[16,2048,128]{2,1,0:T(8,128)(2,1)S(1)} %get-tuple-element.16) | data formatting | bytes 16777216
  208.1 0.6 copy.19
  208.7 0.6 copy.20
  209.3 0.7 copy.21
Async XLA Ops:
  0.6 0.7 copy-start
  1.4 0.7 copy-start.1
  2.0 0.7 copy-start.2

commit v3 on v2

--- a/solution.py
+++ b/solution.py
@@ -11,6 +11,7 @@
 LOAD_SLOTS = 3
 SUM_LAG = 1
 SCALE_LAG = 1
+PIECES = 4
 KEPT = SUM_LAG + SCALE_LAG + 1
 
 
@@ -47,10 +48,10 @@
 
 def kernel(
     n, groups, order,
-    mix, mg, sg, mu, su, rw, rg,
+    mix_at, mg, sg, mu, su, rw_at, rg_at,
     out_g, out_u, sc_g, sc_u, out_r,
-    loaded, merged, stage, sums, sums_in, scale_out, scales_in,
-    load_sem, small_send, sum_sem, scale_sem, bulk_send, bulk_g, bulk_u,
+    mix, rw, rg, loaded, merged, stage, sums, sums_in, first_in, scale_out, scales_in,
+    param_sem, load_sem, small_send, sum_sem, scale_sem, bulk_send, bulk_g, bulk_u,
     r_send, r_plane, r_group,
 ):
     experts, rows, cols = mg.shape
@@ -73,10 +74,20 @@
             for j in which
         ]
 
-    for e in range(min(LOAD_SLOTS, experts)):
+    params = [
+        pltpu.make_async_copy(src, dst, param_sem.at[j])
+        for j, (src, dst) in enumerate(((mix_at, mix), (rw_at, rw), (rg_at, rg)))
+    ]
+    params[0].start()
+    for copy in load(0):
+        copy.start()
+    pl.semaphore_wait(barrier, n - 1 + groups - 1)
+    for e in range(1, min(LOAD_SLOTS, experts)):
         for copy in load(e):
             copy.start()
-    pl.semaphore_wait(barrier, n - 1 + groups - 1)
+    for copy in params[1:]:
+        copy.start()
+    params[0].wait()
 
     def remote(src, dst, send, recv, k):
         return pltpu.make_async_remote_copy(
@@ -84,7 +95,7 @@
             device_id={"shard": partner(me, k)},
         )
 
-    def mix_and_sum(e):
+    def mix_and_sum(e, first=False):
         slot, keep = lax.rem(e, LOAD_SLOTS), lax.rem(e, KEPT)
         m = mix[e]
         rest = 1.0 - m
@@ -104,9 +115,14 @@
             total = jnp.sum(acc, axis=0, keepdims=True)
             for d in range(n):
                 sums[e, d, t : t + 1, :] = total[:, d * width : (d + 1) * width]
-        sums_in[e, 0] = sums[e, me]
-        for k in order:
-            remote(sums.at[e, partner(me, k)], sums_in.at[e, k], small_send.at[0], sum_sem.at[e], k).start()
+        if first:
+            first_in[0] = sums[e]
+            for k in order:
+                remote(sums.at[e], first_in.at[k], small_send.at[2], sum_sem.at[e], k).start()
+        else:
+            sums_in[e, 0] = sums[e, me]
+            for k in order:
+                remote(sums.at[e, partner(me, k)], sums_in.at[e, k], small_send.at[0], sum_sem.at[e], k).start()
 
         @pl.when(e + LOAD_SLOTS < experts)
         def _():
@@ -124,12 +140,25 @@
         for k in order:
             remote(scale_out.at[e], scales_in.at[e, k], small_send.at[1], scale_sem.at[e], k).start()
 
-    def narrow_and_send(e):
-        keep = lax.rem(e, KEPT)
+    def settle_first():
+        arrived = first_in.at[pl.ds(1, n - 1)]
+        pltpu.make_async_copy(arrived, arrived, sum_sem.at[0]).wait()
+        first_in[0] = jnp.sum(first_in[...], axis=0) / total_rows
+        for k in range(n):
+            scales_in[0, k] = first_in[0, partner(me, k)]
+        sc_g[0:1, :] = scales_in[0, 0, 0:1, :]
+        sc_u[0:1, :] = scales_in[0, 0, 1:2, :]
+
+    def await_scales(e):
         arrived = scales_in.at[e, pl.ds(1, n - 1)]
         pltpu.make_async_copy(arrived, arrived, scale_sem.at[e]).wait()
+
+    def narrow_and_send(e, which=(0, 1)):
+        keep = lax.rem(e, KEPT)
         place = pl.ds(pl.multiple_of(me * rows, rows), rows)
-        for t, out, sem in ((0, out_g, bulk_g), (1, out_u, bulk_u)):
+        for t in which:
+            out, sem = ((out_g, bulk_g), (out_u, bulk_u))[t]
+            ready = None
             for k in (*order, 0):
                 at = pl.ds(pl.multiple_of(partner(me, k) * width, width), width)
                 scale = scales_in[e, k, t : t + 1, :]
@@ -138,13 +167,17 @@
                     stage[e, t, k - 1] = narrow
                 else:
                     out[e, place, :] = narrow
-            for k in order:
-                remote(stage.at[e, t, k - 1], out.at[e, place], bulk_send.at[t], sem, k).start()
+                if ready is not None:
+                    ready.start()
+                if k:
+                    ready = remote(stage.at[e, t, k - 1], out.at[e, place], bulk_send.at[t], sem, k)
 
     height = rw.shape[0]
     high = pl.ds(pl.multiple_of(group * height, height), height)
 
     def router_plane():
+        for copy in params[1:]:
+            copy.wait()
         mine = out_r.at[high, pl.ds(pl.multiple_of(me * rows, rows), rows)]
         mine[...] = (rw[...] * rg[...]).astype(jnp.bfloat16)
         for k in order:
@@ -162,18 +195,30 @@
 
     last = experts + SUM_LAG + SCALE_LAG - 1
 
-    @pl.loop(0, last + 1)
+    mix_and_sum(0, first=True)
+
+    @pl.loop(1, last + 1)
     def _(i):
         @pl.when(i < experts)
         def _():
             mix_and_sum(i)
 
-        @pl.when((i >= SUM_LAG) & (i < experts + SUM_LAG))
+        @pl.when(i == 1)
+        def _():
+            settle_first()
+            narrow_and_send(0, (0,))
+
+        @pl.when((i >= SUM_LAG + 1) & (i < experts + SUM_LAG))
         def _():
             settle(i - SUM_LAG)
 
-        @pl.when(i >= SUM_LAG + SCALE_LAG)
-        def _():
+        @pl.when(i == SUM_LAG + SCALE_LAG)
+        def _():
+            narrow_and_send(0, (1,))
+
+        @pl.when(i > SUM_LAG + SCALE_LAG)
+        def _():
+            await_scales(i - SUM_LAG - SCALE_LAG)
             narrow_and_send(i - SUM_LAG - SCALE_LAG)
 
         @pl.when(i == SUM_LAG + SCALE_LAG)
@@ -188,8 +233,10 @@
         pltpu.make_async_copy(ref, ref, sem).wait()
 
     others = pl.ds(0, (n - 1) * rows)
+    finish(first_in.at[pl.ds(1, n - 1)], small_send.at[2])
     for t, half in enumerate((sums_in, scales_in)):
-        finish(half.at[:, pl.ds(1, n - 1)], small_send.at[t])
+        if experts > 1:
+            finish(half.at[pl.ds(1, experts - 1), pl.ds(1, n - 1)], small_send.at[t])
     finish(out_r.at[pl.ds(0, height), others], r_send.at[0])
     if groups > 1:
         for sem in (r_send.at[1], r_group):
@@ -199,34 +246,56 @@
         finish(out.at[:, others], sem)
 
 
+def write_out(*refs):
+    *pairs, sems = refs
+    count = len(pairs) // 2
+    copies = []
+    for j, (src, dst) in enumerate(zip(pairs[:count], pairs[count:])):
+        pieces = PIECES if len(src.shape) == 3 and src.shape[0] % PIECES == 0 else 1
+        size = src.shape[0] // pieces
+        for p in range(pieces):
+            at = pl.ds(p * size, size)
+            copies.append(pltpu.make_async_copy(src.at[at], dst.at[at], sems.at[j, p]))
+    for copy in copies:
+        copy.start()
+    for copy in copies:
+        copy.wait()
+
+
 def fused(n, groups, master_gate, second_gate, master_up, second_up, mix_share, router_weight, router_gain):
     experts, rows, cols = master_gate.shape
     width = cols // n
     per_group = router_weight.shape[1]
     order = sorted(range(1, n), key=lambda k: (k // 2 == 0, -bin(k // 2).count("1"), k % 2, k))
     f32, bf16 = jnp.float32, jnp.bfloat16
+    in_hbm = functools.partial(pltpu.with_memory_space_constraint, memory_space=pltpu.HBM)
     final = pltpu.VMEM((experts, rows * n, width), bf16)
-    scale = jax.ShapeDtypeStruct((experts, width), f32)
-    anywhere = pl.BlockSpec(memory_space=pl.ANY)
+    scale = pltpu.VMEM((experts, width), f32)
+    hbm = pl.BlockSpec(memory_space=pltpu.HBM)
     vmem = pl.BlockSpec(memory_space=pltpu.VMEM)
-    final_gate, final_up, scale_gate, scale_up, router = pl.pallas_call(
+    results = pl.pallas_call(
         functools.partial(kernel, n, groups, order),
         out_shape=(
             final, final, scale, scale,
-            jax.ShapeDtypeStruct((groups * per_group, n * rows), bf16),
+            pltpu.VMEM((groups * per_group, n * rows), bf16),
         ),
-        in_specs=[pl.BlockSpec(memory_space=pltpu.SMEM)] + [anywhere] * 4 + [vmem] * 2,
+        in_specs=[hbm] * 7,
         out_specs=(vmem,) * 5,
         scratch_shapes=[
+            pltpu.SMEM((experts,), f32),
+            pltpu.VMEM((per_group, rows), f32),
+            pltpu.VMEM((1, rows), f32),
             pltpu.VMEM((LOAD_SLOTS, 4, rows, cols), f32),
             pltpu.VMEM((KEPT, 2, rows, cols), f32),
             pltpu.VMEM((experts, 2, n - 1, rows, width), bf16),
             pltpu.VMEM((experts, n, 2, width), f32),
             pltpu.VMEM((experts, n, 2, width), f32),
+            pltpu.VMEM((n, n, 2, width), f32),
             pltpu.VMEM((experts, 2, width), f32),
             pltpu.VMEM((experts, n, 2, width), f32),
+            pltpu.SemaphoreType.DMA((3,)),
             pltpu.SemaphoreType.DMA((LOAD_SLOTS, 4)),
-            pltpu.SemaphoreType.DMA((2,)),
+            pltpu.SemaphoreType.DMA((3,)),
             pltpu.SemaphoreType.DMA((experts,)),
             pltpu.SemaphoreType.DMA((experts,)),
             pltpu.SemaphoreType.DMA((2,)),
@@ -240,10 +309,18 @@
             collective_id=0, has_side_effects=True, vmem_limit_bytes=36 * 2**20
         ),
     )(
-        mix_share, master_gate, second_gate, master_up, second_up,
-        router_weight.T, router_gain[None, :],
+        in_hbm(mix_share), master_gate, second_gate, master_up, second_up,
+        in_hbm(router_weight.T), in_hbm(router_gain[None, :]),
     )
-    return final_gate, final_up, scale_gate, scale_up, router.T
+    *results, router = pl.pallas_call(
+        write_out,
+        out_shape=[jax.ShapeDtypeStruct(x.shape, x.dtype) for x in results],
+        in_specs=[vmem] * len(results),
+        out_specs=[hbm] * len(results),
+        scratch_shapes=[pltpu.SemaphoreType.DMA((len(results), PIECES))],
+        compiler_params=pltpu.CompilerParams(vmem_limit_bytes=2**20),
+    )(*results)
+    return (*results, router.T)
 
 
 def solution(mesh):

time: 210 us -> 202 us (0.962)
  local copies, waits for them, and re-layouts: 10.7 us -> 0 us
  Pallas kernels: 199 us -> 202 us
    unnamed x11 -> x0, local copies, waits for them, and re-layouts: 10.7 us -> none
    pallas_call x0 -> x1, Pallas kernels: none -> 6.06 us  [fused(): pl.pallas_call(write_out, out_shape=[jax.ShapeDtypeStruct(x.shape, x.dtyp...]
    pallas_call x1, Pallas kernels: 199 us -> 196 us  [fused(): pl.pallas_call(functools.partial(kernel, n, groups, order), out_shape=(fi...]
where the time goes in v3:
time: 202 us
  Pallas kernels  202 us (100%)
    pallas_call x1, Pallas kernels, fused(): pl.pallas_call(functools.partial(kernel, n, groups, order), out_shape=(fi...  196 us
    pallas_call x1, Pallas kernels, fused(): pl.pallas_call(write_out, out_shape=[jax.ShapeDtypeStruct(x.shape, x.dtyp...  6.06 us

profile of v3, /device:TPU:0, one launch (start us, length us, event | category | flops | bytes accessed | tf_op | source)
XLA Modules:
  0.0 202.3 jit_solution(12873625518100569719)
XLA Ops:
  0.6 195.6 %shard_map.110 = (bf16[16,2048,128]{2,1,0:T(8,128)(2,1)S(1)}, bf16[16,2048,128]{2,1,0:T(8,128)(2,1)S(1)}, f32[16,128]{1,0:T(8,128)S(1)}, f32[16,128]{1,0:T(8,128)S(1)}, bf16[64,2048]{1,0:T(8,128)(2,1)S(1)}) custom-call(f32[16]{0:T(128)} %mix_at.1, f32[16,256,1024]{2,1,0:T(8,128)} %mg.1, f32[16,256,1024]{2,1,0:T(8,128)} %sg.1, f32[16,256,1024]{2,1,0:T(8,128)} %mu.1, ...), custom_call_target="tpu_custom_call" | custom-call | tf_op jit(solution)/shard_map/pallas_call | solution.py:276
  196.2 6.1 %shard_map.111 = (bf16[16,2048,128]{2,1,0:T(8,128)(2,1)}, bf16[16,2048,128]{2,1,0:T(8,128)(2,1)}, f32[16,128]{1,0:T(8,128)}, f32[16,128]{1,0:T(8,128)}, bf16[64,2048]{1,0:T(8,128)(2,1)}) custom-call(bf16[16,2048,128]{2,1,0:T(8,128)(2,1)S(1)} %get-tuple-element.15.refs_0_, bf16[16,2048,128]{2,1,0:T(8,128)(2,1)S(1)} %get-tuple-element.16.refs_1_, ...), custom_call_target="tpu_custom_call" | custom-call | tf_op jit(solution)/shard_map/pallas_call | solution.py:315
